TPU v7x, 256 devices: a whole 4x4x8 slice. The times are simulated.
256 devices in a mesh: pb: 16 (over x, y), wa: 16 (over z, core).
Axes of the slice: x: 4, y: 4, z: 8, core: 2. Of those that a mesh axis runs over, the one named last changes fastest.
Arguments:
- quartets: int32 [8192, 4, 128], P(('pb', 'wa')), may hold values from -1 to 49151, as said below
- counts: int32 [256], P(('pb', 'wa')), may hold values from 1 to 32, as said below
- eig: bfloat16 [24, 49152], P(None, 'pb'), may hold values from -1.1953125 to 1.1953125
- freq: bfloat16 [49152], P('pb'), may hold values from 0.5 to 2
- phi: bfloat16 [144, 1152], replicated, may hold values from -0.5390625 to 0.5390625
- cells: int32 [8, 9], replicated, may hold values from -2 to 2
Outputs:
- rates: float32 [49152], P(('pb', 'wa'))
Inputs may be any that keep to these rules, and one draw needn't show every extreme that they name: quartets[b, 0, n] is a mode of one of the 256 q-points of the owner group of slot b (from 0 to 3071); the other three entries are all -1 or all modes of the mesh, and then their q-points and that of the first add up as q1 + q2 = q3 + q4 on the mesh. The used slots of a device are its first counts slots; some device has exactly 32.
All inputs are finite; a program needn't handle non-finite values.
Results may differ from a plain program's by a relative error of at most 0.0023.
Values may be sent and summed in bfloat16 or wider, within the bound.
A program may use at most 64 MiB of HBM per device.

v0:
```python
import functools
import math

import jax
import jax.numpy as jnp
from jax import lax
from jax.experimental import pallas as pl
from jax.experimental.pallas import tpu as pltpu
from jax.sharding import PartitionSpec as P

QMESH = 16
BR = 12
NB = 16
LOCAL = 3072
GROUP = 768
LANES = 128
GROUP_AT = (0, 768, 1664, 2432)
FREQ_AT = 1536
WIDTH = 3200
SMEARING = 0.5
MESH = pl.DeviceIdType.MESH
NT = (((1,), (1,)), ((), ()))


ORDER = (
    (-1, 0), (1, 0), (0, -1), (0, 1), (2, 0), (-1, -1), (-1, 1), (0, 2), (1, -1), (1, 1), (-1, 2), (2, -1), (2, 1), (1, 2), (2, 2),
)
WAVES = (
    ((-1, 0), (1, 0), (0, -1), (0, 1)),
    ((2, 0), (0, 2)),
    ((-1, 1), (1, -1)),
    ((-1, -1), (1, 1)),
    ((-1, 2), (2, -1), (2, 1), (1, 2)),
    ((2, 2),),
)
WAVE_AFTER = {5: (0,), 9: (1,), 10: (2,), 12: (3,), 14: (4, 5)}


def wrapped(offset):
    return (offset + 1) % 4 - 1


def hit(rows, columns, where):
    r = lax.broadcasted_iota(jnp.int32, (rows, columns), 0)
    c = lax.broadcasted_iota(jnp.int32, (rows, columns), 1)
    return jnp.where(where(r) == c, 1.0, 0.0).astype(jnp.bfloat16)


def spread_column(r):
    kind = floor_div(r, 144)
    t = r - 144 * kind
    first = floor_div(t, BR)
    return ((kind + 2) & 3) * 16 + jnp.where((kind & 1) == 0, first, t - BR * first)


def order_column(r):
    t = r & 31
    lane = jnp.where(t < 12, t, jnp.where(t == 12, 24, jnp.where((t >= 16) & (t < 28), t - 4, -999)))
    return lane + (r - t)


def exchange_kernel(
    eig, freq, quartets, phi, cells, counts,
    table, blocks, tallies, rows, phi_v, cells_v, reorder, spread,
    tab, mine, eye, dealt, send, got, lent, local,
):
    pb, wa = lax.axis_index("pb"), lax.axis_index("wa")
    x, y, core = pb // 4, pb % 4, wa % 2
    ahead = 1 - 2 * core
    sibling = (pb, wa + ahead)

    def place(dx, dy):
        return lax.rem(x + ahead * dx + 4, 4) * 4 + lax.rem(y + ahead * dy + 4, 4)

    barrier = pltpu.get_barrier_semaphore()
    for step in (1, -1):
        pl.semaphore_signal(barrier, inc=1, device_id=(place(step, 0), wa), device_id_type=MESH)
        pl.semaphore_signal(barrier, inc=1, device_id=(place(0, step), wa), device_id_type=MESH)
    for k in range(1, NB):
        pl.semaphore_signal(barrier, inc=1, device_id=(pb, lax.rem(wa + k, NB)), device_id_type=MESH)

    left = pltpu.make_async_copy(eig.at[:, pl.ds(0, 1536)], tab.at[pb, :, pl.ds(0, 1536)], local.at[0])
    right = pltpu.make_async_copy(eig.at[:, pl.ds(1536, 1536)], tab.at[pb, :, pl.ds(1664, 1536)], local.at[1])
    copy_freq = pltpu.make_async_copy(freq, tab.at[pb, :, pl.ds(FREQ_AT, LANES)], local.at[2])
    copy_dealt = pltpu.make_async_copy(quartets, dealt, local.at[3])
    copy_phi = pltpu.make_async_copy(phi, phi_v, local.at[4])
    copy_cells = pltpu.make_async_copy(cells, cells_v, local.at[5])
    own = (left, right, copy_freq, copy_dealt)
    for copy in own + (copy_phi, copy_cells):
        copy.start()
    mine[...] = jnp.full((1, LANES), counts[0], jnp.int32)
    tallies[wa] = mine[...]
    eye[...] = hit(256, 256, lambda r: r)
    reorder[...] = hit(LANES, LANES, order_column)
    spread[...] = hit(576, 64, spread_column)
    for copy in own:
        copy.wait()
    blocks[wa] = dealt[:, 0]

    pl.semaphore_wait(barrier, 4 + NB - 1)

    def push(src, dst, sent, arrival, device):
        pltpu.make_async_remote_copy(
            src_ref=src, dst_ref=dst, send_sem=send.at[sent], recv_sem=arrival, device_id=device, device_id_type=MESH
        ).start()

    def bytes_in(view, sem):
        pltpu.make_async_remote_copy(
            src_ref=view, dst_ref=view, send_sem=send.at[0], recv_sem=sem, device_id=sibling, device_id_type=MESH
        ).wait_recv()

    def bytes_out(view, sent):
        pltpu.make_async_remote_copy(
            src_ref=view, dst_ref=view, send_sem=send.at[sent], recv_sem=got.at[0], device_id=sibling, device_id_type=MESH
        ).wait_send()

    def at(part, first, second):
        return place(first, second) if part == 0 else place(second, first)

    def relay(part, first, second, axis, step):
        shard = at(part, first, second)
        if part == 0:
            view = tab.at[shard, :, pl.ds(pl.multiple_of(core * 2432, LANES), 768)]
        else:
            view = tab.at[shard, :, pl.ds(pl.multiple_of(768 + core * 768, LANES), 896)]
        key = (wrapped(first - step), second) if axis == 0 else (first, wrapped(second - step))
        target = at(part, step, 0) if axis == 0 else at(part, 0, step)
        push(view, view, part, got.at[ORDER.index(key)], (target, wa))

    def lend(part, first, second):
        shard = at(part, first, second)
        if part == 0:
            view = tab.at[shard, :, pl.ds(pl.multiple_of(core * 2432, LANES), 768)]
        else:
            view = tab.at[shard, :, pl.ds(pl.multiple_of(768 + core * 896, LANES), 768)]
        offset = (first, second) if part == 0 else (second, first)
        wave = [w for w, members in enumerate(WAVES) if offset in members][0]
        push(view, view, 2, lent.at[wave], sibling)

    def turn(shard):
        values = tab[shard, :, FREQ_AT : FREQ_AT + LANES].astype(jnp.float32)
        for j in range(3):
            stack = []
            for g in range(4):
                stack.append(tab[shard, :, GROUP_AT[g] + 256 * j : GROUP_AT[g] + 256 * (j + 1)].astype(jnp.float32))
                at_row = 6 * g + 2 * j
                stack.append(
                    jnp.concatenate(
                        [jnp.broadcast_to(values[at_row + h : at_row + h + 1, :], (8, LANES)) for h in range(2)], axis=1
                    )
                )
            stack = jnp.concatenate(stack, axis=0).astype(jnp.bfloat16)
            table[pl.ds(pl.multiple_of(shard * GROUP + 256 * j, 256), 256), :] = lax.dot_general(
                eye[...], stack, NT, preferred_element_type=jnp.float32
            )

    for axis in (0, 1):
        for part in (0, 1):
            relay(part, 0, 0, axis, 1)
            relay(part, 0, 0, axis, -1)
    for k in range(1, NB):
        peer = lax.rem(wa + k, NB)
        push(dealt.at[:, k], blocks.at[wa], 3, lent.at[len(WAVES)], (pb, peer))
        push(mine, tallies.at[wa], 4, lent.at[len(WAVES) + 1], (pb, peer))
    turn(pb)

    for number, (first, second) in enumerate(ORDER):
        bytes_in(tab.at[0, :, pl.ds(0, 1664)], got.at[number])
        for part in (0, 1):
            if second == 0:
                if first == -1:
                    relay(part, first, 0, 0, 1)
                relay(part, first, 0, 1, 1)
                relay(part, first, 0, 1, -1)
            elif second == -1:
                relay(part, first, second, 1, 1)
            lend(part, first, second)
        if number == 7:
            bytes_in(blocks.at[pl.ds(0, NB - 1)], lent.at[len(WAVES)])
            bytes_in(tallies.at[pl.ds(0, NB - 1)], lent.at[len(WAVES) + 1])
            modes = jnp.maximum(blocks[...], 0)
            local_mode = lax.broadcasted_iota(jnp.int32, modes.shape, 2) == 0
            rows[...] = rows_of(modes + jnp.where(local_mode, pb * LOCAL, 0))
        for wave in WAVE_AFTER.get(number, ()):
            members = WAVES[wave]
            bytes_in(tab.at[pl.ds(0, len(members)), :, pl.ds(0, 1536)], lent.at[wave])
            for offset in members:
                turn(place(*offset))

    copy_phi.wait()
    copy_cells.wait()
    bytes_out(tab.at[pl.ds(0, 15), :, pl.ds(0, 768)], 0)
    bytes_out(tab.at[pl.ds(0, 15), :, pl.ds(0, 896)], 1)
    bytes_out(tab.at[pl.ds(0, 15), :, pl.ds(0, 1536)], 2)
    bytes_out(blocks.at[pl.ds(0, NB - 1)], 3)
    bytes_out(tallies.at[pl.ds(0, NB - 1)], 4)


def exchange(eig, freq, quartets, phi, cells, counts):
    hbm = pl.BlockSpec(memory_space=pltpu.HBM)
    vmem = pl.BlockSpec(memory_space=pltpu.VMEM)
    return pl.pallas_call(
        exchange_kernel,
        out_shape=(
            pltpu.VMEM((NB * GROUP, LANES), jnp.float32),
            pltpu.VMEM((NB, 2, 4, LANES), jnp.int32),
            pltpu.VMEM((NB, 1, LANES), jnp.int32),
            pltpu.VMEM((NB, 2, 4, LANES), jnp.int32),
            pltpu.VMEM((144, 1152), jnp.bfloat16),
            pltpu.VMEM((8, 9), jnp.int32),
            pltpu.VMEM((128, 128), jnp.bfloat16),
            pltpu.VMEM((576, 64), jnp.bfloat16),
        ),
        in_specs=[hbm] * 5 + [pl.BlockSpec(memory_space=pltpu.SMEM)],
        out_specs=(vmem,) * 8,
        scratch_shapes=[
            pltpu.VMEM((NB, 24, WIDTH), jnp.bfloat16),
            pltpu.VMEM((1, LANES), jnp.int32),
            pltpu.VMEM((256, 256), jnp.bfloat16),
            pltpu.VMEM((2, NB, 4, LANES), jnp.int32),
            pltpu.SemaphoreType.DMA((5,)),
            pltpu.SemaphoreType.DMA((len(ORDER),)),
            pltpu.SemaphoreType.DMA((len(WAVES) + 2,)),
            pltpu.SemaphoreType.DMA((6,)),
        ],
        compiler_params=pltpu.CompilerParams(collective_id=0, has_side_effects=True, vmem_limit_bytes=24 << 20),
        name="exchange",
    )(*[pltpu.with_memory_space_constraint(a, pltpu.HBM) for a in (eig, freq, quartets, phi, cells)], counts)


def cosine_of(step):
    near = jnp.minimum(step, 16 - step)
    out = jnp.full(step.shape, -1.0, jnp.float32)
    for k in range(8):
        out = jnp.where(near == k, math.cos(math.pi * k / 8) if k != 4 else 0.0, out)
    return out


def floor_div(value, by):
    return jnp.floor((value.astype(jnp.float32) + 0.5) * (1.0 / by)).astype(jnp.int32)


def rows_of(modes):
    unit = floor_div(modes, GROUP)
    return (unit >> 2) * GROUP + modes - unit * GROUP


def quartet_kernel(
    table, blocks, tallies, rows, phi, cells, reorder, spread, out,
    wide_a, wide_b, near_a, near_b, scale_a, scale_b, held_a, held_b, rows_a, rows_b, tally_s, live_s, sums, sem,
):
    pb, wa = lax.axis_index("pb"), lax.axis_index("wa")
    copy_tally = pltpu.make_async_copy(tallies, tally_s, sem.at[2])
    copy_tally.start()
    sums[...] = jnp.zeros_like(sums)
    cell = cells[...].astype(jnp.float32)
    copy_tally.wait()

    live_s[0] = 0
    total = jnp.int32(0)
    for source in range(NB):
        held = (wa - source) & (NB - 1)
        tally = tally_s[source, 0, 0]
        for high in range(2):
            live_s[total] = 2 * source + high
            total = total + (held + NB * high < tally).astype(jnp.int32)
    for k in range(6):
        live_s[total + k] = 0

    def fetch(index, into, which):
        slot = live_s[index]
        return pltpu.make_async_copy(rows.at[slot >> 1, slot & 1], into, sem.at[which])

    def gather(into, at):
        for n in range(LANES):
            for k in range(4):
                into[LANES * k + n : LANES * k + n + 1, :] = table[pl.ds(at[k, n], 1), :]

    def products(held, index, wide, near, scale):
        slot = live_s[index]
        raw = blocks[slot >> 1, slot & 1]
        modes = jnp.maximum(raw, 0)
        fullmode = modes + jnp.where(lax.broadcasted_iota(jnp.int32, modes.shape, 0) == 0, pb * LOCAL, 0)
        group = floor_div(fullmode, GROUP) & 3
        turned = lax.dot_general(reorder[...], held[...].astype(jnp.bfloat16), NT, preferred_element_type=jnp.float32)
        halves, freqs = [], []
        for k in range(4):
            which = group[k : k + 1, :]
            part = turned[:, LANES * k : LANES * (k + 1)]
            mine = jnp.where(
                which < 2,
                jnp.where(which == 0, part[0:32], part[32:64]),
                jnp.where(which == 2, part[64:96], part[96:128]),
            )
            halves.append(jnp.concatenate([mine[0:16], mine[16:32]], axis=1))
            freqs.append(mine[12:13])
        vectors = jnp.concatenate(halves, axis=0).astype(jnp.bfloat16)
        pairs = jnp.dot(spread[...], vectors, preferred_element_type=jnp.float32)
        third, fourth, e1, e2 = (pairs[144 * k : 144 * (k + 1)] for k in range(4))
        far_re = third[:, :LANES] * fourth[:, :LANES] - third[:, LANES:] * fourth[:, LANES:]
        far_im = -(third[:, :LANES] * fourth[:, LANES:] + third[:, LANES:] * fourth[:, :LANES])
        near[0:144] = e1[:, :LANES] * e2[:, :LANES] - e1[:, LANES:] * e2[:, LANES:]
        near[144:288] = e1[:, :LANES] * e2[:, LANES:] + e1[:, LANES:] * e2[:, :LANES]

        point = floor_div(modes, BR)
        coords = [(point >> 8).astype(jnp.float32), ((point >> 4) & 15).astype(jnp.float32), (point & 15).astype(jnp.float32)]
        shift = jnp.zeros((8, LANES), jnp.float32)
        for which in range(3):
            for axis in range(3):
                column = cell[:, 3 * which + axis : 3 * which + axis + 1]
                term = column * coords[axis][which + 1 : which + 2, :]
                shift = shift + term if which == 0 else shift - term
        step = shift.astype(jnp.int32) & 15
        cosine, sine = cosine_of(step), cosine_of((step - 4) & 15)
        for k in range(8):
            c, s = cosine[k : k + 1, :], sine[k : k + 1, :]
            wide[144 * k : 144 * (k + 1), :LANES] = (c * far_re - s * far_im).astype(jnp.bfloat16)
            wide[144 * k : 144 * (k + 1), LANES:] = (c * far_im + s * far_re).astype(jnp.bfloat16)

        occupied = [1.0 / (jnp.exp(f) - 1.0) for f in freqs]
        mismatch = freqs[0] + freqs[1] - freqs[2] - freqs[3]
        delta = jnp.exp(-((mismatch / SMEARING) ** 2)) / (SMEARING * math.sqrt(math.pi))
        weight = (1.0 + occupied[1]) * occupied[2] * occupied[3] / occupied[0]
        product = freqs[0] * freqs[1] * freqs[2] * freqs[3]
        valid = (raw[1:2, :] >= 0) & (index < total)
        scale[...] = jnp.where(valid, delta * weight / product, 0.0)

    def contract(index, wide, near, scale):
        slot = live_s[index]
        weighted = jnp.dot(phi[...], wide[...], preferred_element_type=jnp.float32)
        w_re, w_im = weighted[:, :LANES], weighted[:, LANES:]
        near_re, near_im = near[0:144], near[144:288]
        value_re = jnp.sum(near_re * w_re - near_im * w_im, axis=0, keepdims=True)
        value_im = jnp.sum(near_re * w_im + near_im * w_re, axis=0, keepdims=True)
        term = (value_re * value_re + value_im * value_im) * scale[...]

        first = jnp.maximum(blocks[slot >> 1, slot & 1][0:1, :], 0)
        high = floor_div(first, 192)
        low = first - 192 * high
        placed = jnp.where(lax.broadcasted_iota(jnp.int32, (NB, LANES), 0) == high, term, 0.0)
        one = placed.astype(jnp.bfloat16)
        rest = placed - one.astype(jnp.float32)
        two = rest.astype(jnp.bfloat16)
        three = (rest - two.astype(jnp.float32)).astype(jnp.bfloat16)
        spot = jnp.where(lax.broadcasted_iota(jnp.int32, (256, LANES), 0) == low, 1.0, 0.0).astype(jnp.bfloat16)
        sums[...] += lax.dot_general(
            jnp.concatenate([one, two, three], axis=0), spot, NT, preferred_element_type=jnp.float32
        )

    fetch(0, rows_a, 0).start()
    fetch(1, rows_b, 1).start()
    fetch(0, rows_a, 0).wait()
    gather(held_a, rows_a)
    fetch(2, rows_a, 0).start()
    fetch(1, rows_b, 1).wait()
    gather(held_b, rows_b)
    products(held_a, 0, wide_a, near_a, scale_a)
    fetch(3, rows_b, 1).start()

    def two_blocks(it, carry):
        i = 2 * it
        fetch(i + 2, rows_a, 0).wait()
        gather(held_a, rows_a)
        products(held_b, i + 1, wide_b, near_b, scale_b)
        contract(i, wide_a, near_a, scale_a)
        fetch(i + 4, rows_a, 0).start()
        fetch(i + 3, rows_b, 1).wait()
        gather(held_b, rows_b)
        products(held_a, i + 2, wide_a, near_a, scale_a)
        contract(i + 1, wide_b, near_b, scale_b)
        fetch(i + 5, rows_b, 1).start()
        return carry

    trips = (total + 1) // 2
    lax.fori_loop(0, trips, two_blocks, 0)
    fetch(2 * trips + 2, rows_a, 0).wait()
    fetch(2 * trips + 3, rows_b, 1).wait()
    result = sums[0:16] + sums[16:32] + sums[32:48]
    for w in range(NB):
        out[w] = result[w : w + 1]


def quartet_sums(*operands):
    vmem = pl.BlockSpec(memory_space=pltpu.VMEM)
    pinned = [pltpu.with_memory_space_constraint(a, pltpu.VMEM) for a in operands]
    return pl.pallas_call(
        quartet_kernel,
        out_shape=pltpu.VMEM((NB, 1, 256), jnp.float32),
        in_specs=[vmem] * 8,
        out_specs=vmem,
        scratch_shapes=[
            pltpu.VMEM((1152, 256), jnp.bfloat16),
            pltpu.VMEM((1152, 256), jnp.bfloat16),
            pltpu.VMEM((288, LANES), jnp.float32),
            pltpu.VMEM((288, LANES), jnp.float32),
            pltpu.VMEM((1, LANES), jnp.float32),
            pltpu.VMEM((1, LANES), jnp.float32),
            pltpu.VMEM((4 * LANES, LANES), jnp.float32),
            pltpu.VMEM((4 * LANES, LANES), jnp.float32),
            pltpu.SMEM((4, LANES), jnp.int32),
            pltpu.SMEM((4, LANES), jnp.int32),
            pltpu.SMEM((NB, 1, LANES), jnp.int32),
            pltpu.SMEM((2 * NB + 8,), jnp.int32),
            pltpu.VMEM((48, 256), jnp.float32),
            pltpu.SemaphoreType.DMA((3,)),
        ],
        compiler_params=pltpu.CompilerParams(vmem_limit_bytes=16 << 20),
        name="quartets",
    )(*pinned)


def reduce_kernel(part, out, arrived, send, recv):
    pb, wa = lax.axis_index("pb"), lax.axis_index("wa")
    barrier = pltpu.get_barrier_semaphore()
    peers = [lax.rem(wa + k, NB) for k in range(1, NB)]
    for peer in peers:
        pl.semaphore_signal(barrier, inc=1, device_id=(pb, peer), device_id_type=MESH)
    pl.semaphore_wait(barrier, NB - 1)
    for k, peer in enumerate(peers):
        pltpu.make_async_remote_copy(
            src_ref=part.at[peer], dst_ref=arrived.at[k], send_sem=send.at[0], recv_sem=recv.at[0],
            device_id=(pb, peer), device_id_type=MESH,
        ).start()
    everything = pltpu.make_async_remote_copy(
        src_ref=part.at[pl.ds(0, NB - 1)], dst_ref=arrived, send_sem=send.at[0], recv_sem=recv.at[0],
        device_id=(pb, peers[0]), device_id_type=MESH,
    )
    everything.wait_recv()
    total = part[wa]
    for k in range(NB - 1):
        total = total + arrived[k]
    out[...] = total
    everything.wait_send()


def reduce_over_wa(part):
    vmem = pl.BlockSpec(memory_space=pltpu.VMEM)
    return pl.pallas_call(
        reduce_kernel,
        out_shape=jax.ShapeDtypeStruct((1, 256), jnp.float32),
        in_specs=[vmem],
        out_specs=vmem,
        scratch_shapes=[
            pltpu.VMEM((NB - 1, 1, 256), jnp.float32),
            pltpu.SemaphoreType.DMA((1,)),
            pltpu.SemaphoreType.DMA((1,)),
        ],
        compiler_params=pltpu.CompilerParams(collective_id=1, has_side_effects=True, vmem_limit_bytes=1 << 20),
        name="reduce_wa",
    )(pltpu.with_memory_space_constraint(part, pltpu.VMEM))


def body(quartets, counts, eig, freq, phi, cells):
    dealt = quartets.reshape(2, NB, 4, LANES)
    held = exchange(eig, freq.reshape(24, LANES), dealt, phi, cells, counts)
    part = quartet_sums(*held)
    return reduce_over_wa(part)[0, :192]


def solution(mesh):
    placed = (P(("pb", "wa"), None, None), P(("pb", "wa")), P(None, "pb"), P("pb"), P(), P())
    return jax.shard_map(body, mesh=mesh, in_specs=placed, out_specs=P(("pb", "wa")), check_vma=False)
```

profile of v0, /device:TPU:1, one launch (start us, length us, event | category | flops | bytes accessed | tf_op | source)
XLA Modules:
  0.0 47.8 jit_solution(10538334251170656125)
XLA Ops:
  0.7 27.2 %exchange.1 = (f32[12288,128]{1,0:T(8,128)S(1)}, s32[16,2,4,128]{3,2,1,0:T(4,128)S(1)}, s32[16,1,128]{2,1,0:T(1,128)S(1)}, s32[16,2,4,128]{3,2,1,0:T(4,128)S(1)}...) custom-call(bf16[24,3072]{1,0:T(8,128)(2,1)} %eig.1, ...), custom_call_target="tpu_custom_call" | custom-call | tf_op jit(solution)/shard_map/exchange/pallas_call | solution.py:202
  27.9 11.7 %quartets.1.part = f32[16,1,256]{2,1,0:T(1,128)S(1)} custom-call(f32[12288,128]{1,0:T(8,128)S(1)} %get-tuple-element.13.table, s32[16,2,4,128]{3,2,1,0:T(4,128)S(1)} %get-tuple-element.14.blocks, s32[16,1,128]{2,1,0:T(1,128)S(1)} %get-tuple-element.15.tallies, s32[16,2,4,128]{3,2,1,0:T(4,128)S(1)} %get-tuple-element.16.rows, ...), custom_call_target="tpu_custom_call" | custom-call | tf_op jit(solution)/shard_map/quartets/pallas_call | solution.py:386
  39.6 7.6 %reduce_wa.1 = f32[1,256]{1,0:T(1,128)S(1)} custom-call(f32[16,1,256]{2,1,0:T(1,128)S(1)} %quartets.1.part), custom_call_target="tpu_custom_call" | custom-call | tf_op jit(solution)/shard_map/reduce_wa/pallas_call | solution.py:438
  47.2 0.6 %copy.9 = f32[192]{0:T(256)} copy(f32[192]{0:T(256)S(1)} %bitcast.4) | data formatting | bytes 1536
where the time goes:
time: 47.8 us
  Pallas kernels  46.6 us (97%)
  between operations  0.68 us (1%)
  local copies, waits for them, and re-layouts  0.56 us (1%)
    pallas_call x1, Pallas kernels, exchange(): pl.pallas_call(exchange_kernel, out_shape=(pltpu.VMEM((NB * GROUP, LANES)...  27.2 us
    pallas_call x1, Pallas kernels, quartet_sums(): pl.pallas_call(quartet_kernel, out_shape=pltpu.VMEM((NB, 1, 256), jnp.flo...  11.7 us
    pallas_call x1, Pallas kernels, reduce_over_wa(): pl.pallas_call(reduce_kernel, out_shape=jax.ShapeDtypeStruct((1, 256), jn...  7.62 us

commit v1 on v0

--- a/solution.py
+++ b/solution.py
@@ -247,7 +247,8 @@
 
 def quartet_kernel(
     table, blocks, tallies, rows, phi, cells, reorder, spread, out,
-    wide_a, wide_b, near_a, near_b, scale_a, scale_b, held_a, held_b, rows_a, rows_b, tally_s, live_s, sums, sem,
+    wide_a, wide_b, near_a, near_b, scale_a, scale_b, term_a, term_b, vectors_a, vectors_b, held_a, held_b,
+    rows_a, rows_b, tally_s, live_s, sums, sem,
 ):
     pb, wa = lax.axis_index("pb"), lax.axis_index("wa")
     copy_tally = pltpu.make_async_copy(tallies, tally_s, sem.at[2])
@@ -271,18 +272,28 @@
         slot = live_s[index]
         return pltpu.make_async_copy(rows.at[slot >> 1, slot & 1], into, sem.at[which])
 
+    sublane = lax.broadcasted_iota(jnp.int32, (8, LANES), 0)
+    odd = [(sublane & (1 << bit)) != 0 for bit in range(3)]
+
     def gather(into, at):
-        for n in range(LANES):
-            for k in range(4):
-                into[LANES * k + n : LANES * k + n + 1, :] = table[pl.ds(at[k, n], 1), :]
-
-    def products(held, index, wide, near, scale):
+        for k in range(4):
+            for n in range(0, LANES, 16):
+                pair = []
+                for half in (n, n + 8):
+                    level = [table[pl.ds(at[k, half + j], 8, stride=0), :] for j in range(8)]
+                    for bit in range(3):
+                        level = [jnp.where(odd[bit], high, low) for low, high in zip(level[::2], level[1::2])]
+                    pair.append(level[0])
+                into[LANES * k + n : LANES * k + n + 16, :] = jnp.concatenate(pair, axis=0).astype(jnp.bfloat16)
+
+    def vectors_of(at, index, held, vectors, scale):
+        gather(held, at)
         slot = live_s[index]
         raw = blocks[slot >> 1, slot & 1]
         modes = jnp.maximum(raw, 0)
         fullmode = modes + jnp.where(lax.broadcasted_iota(jnp.int32, modes.shape, 0) == 0, pb * LOCAL, 0)
         group = floor_div(fullmode, GROUP) & 3
-        turned = lax.dot_general(reorder[...], held[...].astype(jnp.bfloat16), NT, preferred_element_type=jnp.float32)
+        turned = lax.dot_general(reorder[...], held[...], NT, preferred_element_type=jnp.float32)
         halves, freqs = [], []
         for k in range(4):
             which = group[k : k + 1, :]
@@ -294,8 +305,19 @@
             )
             halves.append(jnp.concatenate([mine[0:16], mine[16:32]], axis=1))
             freqs.append(mine[12:13])
-        vectors = jnp.concatenate(halves, axis=0).astype(jnp.bfloat16)
-        pairs = jnp.dot(spread[...], vectors, preferred_element_type=jnp.float32)
+        vectors[...] = jnp.concatenate(halves, axis=0).astype(jnp.bfloat16)
+        occupied = [1.0 / (jnp.exp(f) - 1.0) for f in freqs]
+        mismatch = freqs[0] + freqs[1] - freqs[2] - freqs[3]
+        delta = jnp.exp(-((mismatch / SMEARING) ** 2)) / (SMEARING * math.sqrt(math.pi))
+        weight = (1.0 + occupied[1]) * occupied[2] * occupied[3] / occupied[0]
+        product = freqs[0] * freqs[1] * freqs[2] * freqs[3]
+        valid = (raw[1:2, :] >= 0) & (index < total)
+        scale[...] = jnp.where(valid, delta * weight / product, 0.0)
+
+    def products(index, vectors, wide, near):
+        slot = live_s[index]
+        modes = jnp.maximum(blocks[slot >> 1, slot & 1], 0)
+        pairs = jnp.dot(spread[...], vectors[...], preferred_element_type=jnp.float32)
         third, fourth, e1, e2 = (pairs[144 * k : 144 * (k + 1)] for k in range(4))
         far_re = third[:, :LANES] * fourth[:, :LANES] - third[:, LANES:] * fourth[:, LANES:]
         far_im = -(third[:, :LANES] * fourth[:, LANES:] + third[:, LANES:] * fourth[:, :LANES])
@@ -317,23 +339,16 @@
             wide[144 * k : 144 * (k + 1), :LANES] = (c * far_re - s * far_im).astype(jnp.bfloat16)
             wide[144 * k : 144 * (k + 1), LANES:] = (c * far_im + s * far_re).astype(jnp.bfloat16)
 
-        occupied = [1.0 / (jnp.exp(f) - 1.0) for f in freqs]
-        mismatch = freqs[0] + freqs[1] - freqs[2] - freqs[3]
-        delta = jnp.exp(-((mismatch / SMEARING) ** 2)) / (SMEARING * math.sqrt(math.pi))
-        weight = (1.0 + occupied[1]) * occupied[2] * occupied[3] / occupied[0]
-        product = freqs[0] * freqs[1] * freqs[2] * freqs[3]
-        valid = (raw[1:2, :] >= 0) & (index < total)
-        scale[...] = jnp.where(valid, delta * weight / product, 0.0)
-
-    def contract(index, wide, near, scale):
-        slot = live_s[index]
+    def contract(wide, near, scale, term):
         weighted = jnp.dot(phi[...], wide[...], preferred_element_type=jnp.float32)
         w_re, w_im = weighted[:, :LANES], weighted[:, LANES:]
         near_re, near_im = near[0:144], near[144:288]
         value_re = jnp.sum(near_re * w_re - near_im * w_im, axis=0, keepdims=True)
         value_im = jnp.sum(near_re * w_im + near_im * w_re, axis=0, keepdims=True)
-        term = (value_re * value_re + value_im * value_im) * scale[...]
-
+        term[...] = (value_re * value_re + value_im * value_im) * scale[...]
+
+    def scatter(index, term):
+        slot = live_s[index]
         first = jnp.maximum(blocks[slot >> 1, slot & 1][0:1, :], 0)
         high = floor_div(first, 192)
         low = first - 192 * high
@@ -347,34 +362,45 @@
             jnp.concatenate([one, two, three], axis=0), spot, NT, preferred_element_type=jnp.float32
         )
 
+    sides = (
+        (rows_a, held_a, vectors_a, scale_a, wide_a, near_a, term_a, 0),
+        (rows_b, held_b, vectors_b, scale_b, wide_b, near_b, term_b, 1),
+    )
+
+    def step_of(i, side):
+        at, held, vectors, scale, wide, near, term, which = sides[side]
+        _, _, next_vectors, _, next_wide, next_near, last_term, _ = sides[1 - side]
+        fetch(i + 2, at, which).wait()
+        scatter(jnp.maximum(i - 1, 0), last_term[...])
+        contract(wide, near, scale, term)
+        products(i + 1, next_vectors, next_wide, next_near)
+        vectors_of(at, i + 2, held, vectors, scale)
+        fetch(i + 4, at, which).start()
+
+    term_b[...] = jnp.zeros_like(term_b)
     fetch(0, rows_a, 0).start()
     fetch(1, rows_b, 1).start()
     fetch(0, rows_a, 0).wait()
-    gather(held_a, rows_a)
+    vectors_of(rows_a, 0, held_a, vectors_a, scale_a)
     fetch(2, rows_a, 0).start()
     fetch(1, rows_b, 1).wait()
-    gather(held_b, rows_b)
-    products(held_a, 0, wide_a, near_a, scale_a)
+    products(0, vectors_a, wide_a, near_a)
+    vectors_of(rows_b, 1, held_b, vectors_b, scale_b)
     fetch(3, rows_b, 1).start()
 
     def two_blocks(it, carry):
-        i = 2 * it
-        fetch(i + 2, rows_a, 0).wait()
-        gather(held_a, rows_a)
-        products(held_b, i + 1, wide_b, near_b, scale_b)
-        contract(i, wide_a, near_a, scale_a)
-        fetch(i + 4, rows_a, 0).start()
-        fetch(i + 3, rows_b, 1).wait()
-        gather(held_b, rows_b)
-        products(held_a, i + 2, wide_a, near_a, scale_a)
-        contract(i + 1, wide_b, near_b, scale_b)
-        fetch(i + 5, rows_b, 1).start()
+        step_of(2 * it, 0)
+
+        @pl.when(2 * it + 1 < total)
+        def _():
+            step_of(2 * it + 1, 1)
+
         return carry
 
-    trips = (total + 1) // 2
-    lax.fori_loop(0, trips, two_blocks, 0)
-    fetch(2 * trips + 2, rows_a, 0).wait()
-    fetch(2 * trips + 3, rows_b, 1).wait()
+    lax.fori_loop(0, (total + 1) // 2, two_blocks, 0)
+    scatter(total - 1, jnp.where(total % 2 == 1, term_a[...], term_b[...]))
+    fetch(0, rows_a, 0).wait()
+    fetch(0, rows_b, 1).wait()
     result = sums[0:16] + sums[16:32] + sums[32:48]
     for w in range(NB):
         out[w] = result[w : w + 1]
@@ -395,8 +421,12 @@
             pltpu.VMEM((288, LANES), jnp.float32),
             pltpu.VMEM((1, LANES), jnp.float32),
             pltpu.VMEM((1, LANES), jnp.float32),
-            pltpu.VMEM((4 * LANES, LANES), jnp.float32),
-            pltpu.VMEM((4 * LANES, LANES), jnp.float32),
+            pltpu.VMEM((1, LANES), jnp.float32),
+            pltpu.VMEM((1, LANES), jnp.float32),
+            pltpu.VMEM((64, 256), jnp.bfloat16),
+            pltpu.VMEM((64, 256), jnp.bfloat16),
+            pltpu.VMEM((4 * LANES, LANES), jnp.bfloat16),
+            pltpu.VMEM((4 * LANES, LANES), jnp.bfloat16),
             pltpu.SMEM((4, LANES), jnp.int32),
             pltpu.SMEM((4, LANES), jnp.int32),
             pltpu.SMEM((NB, 1, LANES), jnp.int32),

time: 47.8 us -> 45.5 us (0.952)
  the two profiles are of different devices: /device:TPU:1 before, /device:TPU:3 now
where the time goes in v1:
time: 45.5 us; the launch traced here: 45.7 us
  Pallas kernels  44.4 us (98%)
  between operations  0.68 us (1%)
  local copies, waits for them, and re-layouts  0.56 us (1%)
    pallas_call x1, Pallas kernels, exchange(): pl.pallas_call(exchange_kernel, out_shape=(pltpu.VMEM((NB * GROUP, LANES)...  26.3 us
    pallas_call x1, Pallas kernels, quartet_sums(): pl.pallas_call(quartet_kernel, out_shape=pltpu.VMEM((NB, 1, 256), jnp.flo...  10.5 us
    pallas_call x1, Pallas kernels, reduce_over_wa(): pl.pallas_call(reduce_kernel, out_shape=jax.ShapeDtypeStruct((1, 256), jn...  7.62 us

profile of v1, /device:TPU:3, one launch (start us, length us, event | category | flops | bytes accessed | tf_op | source)
XLA Modules:
  0.0 45.7 jit_solution(8503449856406844319)
XLA Ops:
  0.7 26.3 %exchange.1 = (f32[12288,128]{1,0:T(8,128)S(1)}, s32[16,2,4,128]{3,2,1,0:T(4,128)S(1)}, s32[16,1,128]{2,1,0:T(1,128)S(1)}, s32[16,2,4,128]{3,2,1,0:T(4,128)S(1)}...) custom-call(bf16[24,3072]{1,0:T(8,128)(2,1)} %eig.1, ...), custom_call_target="tpu_custom_call" | custom-call | tf_op jit(solution)/shard_map/exchange/pallas_call | solution.py:202
  27.0 10.5 %quartets.1.part = f32[16,1,256]{2,1,0:T(1,128)S(1)} custom-call(f32[12288,128]{1,0:T(8,128)S(1)} %get-tuple-element.13.table, s32[16,2,4,128]{3,2,1,0:T(4,128)S(1)} %get-tuple-element.14.blocks, s32[16,1,128]{2,1,0:T(1,128)S(1)} %get-tuple-element.15.tallies, s32[16,2,4,128]{3,2,1,0:T(4,128)S(1)} %get-tuple-element.16.rows, ...), custom_call_target="tpu_custom_call" | custom-call | tf_op jit(solution)/shard_map/quartets/pallas_call | solution.py:412
  37.5 7.6 %reduce_wa.1 = f32[1,256]{1,0:T(1,128)S(1)} custom-call(f32[16,1,256]{2,1,0:T(1,128)S(1)} %quartets.1.part), custom_call_target="tpu_custom_call" | custom-call | tf_op jit(solution)/shard_map/reduce_wa/pallas_call | solution.py:468
  45.1 0.6 %copy.9 = f32[192]{0:T(256)} copy(f32[192]{0:T(256)S(1)} %bitcast.4) | data formatting | bytes 1536
